TPU v7x, 32 devices: a whole 2x2x4 slice. The times are simulated.
32 devices in a mesh: groups: 2 (over y), tensor: 4 (over z), frames: 4 (over x, core).
Axes of the slice: x: 2, y: 2, z: 4, core: 2. Of those that a mesh axis runs over, the one named last changes fastest.
Arguments:
- patches: bfloat16 [256, 16, 3072], P('tensor', ('groups', 'frames')), parts along dimension 1, may hold values from -12 to 12
- ln_gain: float32 [3072], replicated, may hold values from 0.5 to 1.5
- in_weight: bfloat16 [3072, 4, 768], P('frames', 'tensor'), may hold values from -0.109375 to 0.109375
- q_gain: float32 [4, 128], P('tensor'), may hold values from 0.1 to 1.9
- k_gain: float32 [4, 128], P('tensor'), may hold values from 0.1 to 1.9
- out_weight: bfloat16 [4, 512, 3072], P('tensor', None, 'frames'), may hold values from -0.25 to 0.25
Outputs:
- encoded: bfloat16 [256, 16, 3072], P('tensor', ('groups', 'frames')), parts along dimension 1
There are 2 independent parts, one for each index of `groups`. A program takes and returns all parts, laid end to end along the dimension named above; an argument that names none is the same for every part. Nothing has to cross between parts.
All inputs are finite; a program needn't handle non-finite values.
Results may differ from a plain program's by a relative error of at most 0.022.
Values may be sent and summed in bfloat16 or wider, within the bound.
No kernel may reach another device: no remote copies, remote signals or barrier semaphores. Data moves between devices by JAX's collectives and lax.ppermute only.
A program may use at most 64 MiB of HBM per device.

v0:
```python
import math
import jax
import jax.numpy as jnp
from jax import lax
from jax.sharding import PartitionSpec as P


def layer_norm(values, gain_vec):
    mean_val = jnp.mean(values, axis=-1, keepdims=True)
    centered = values - mean_val
    variance = jnp.mean(centered * centered, axis=-1, keepdims=True)
    return centered * lax.rsqrt(variance + 1e-06) * gain_vec


def local(patches, ln_gain, in_weight, q_gain, k_gain, out_weight):
    head_dim = q_gain.shape[1]
    normed = layer_norm(patches.astype(jnp.float32), ln_gain).astype(jnp.bfloat16)
    in_local = in_weight[:, 0, :]
    out_local = out_weight[0]
    every_patch = lax.all_gather(normed, "tensor", axis=0, tiled=True)
    joined_cols = jnp.einsum(
        "qye,ea->qya",
        every_patch,
        lax.all_gather(in_local, "frames", axis=0, tiled=True),
        preferred_element_type=jnp.float32,
    )
    query_slice = layer_norm(joined_cols[..., :head_dim], q_gain[0])
    key_slice = layer_norm(joined_cols[..., head_dim : 2 * head_dim], k_gain[0])
    value_slice = joined_cols[..., 2 * head_dim : 3 * head_dim]
    hidden = jax.nn.gelu(joined_cols[..., 3 * head_dim :], approximate=False)
    prepared = jnp.concatenate([query_slice, key_slice, value_slice, hidden], axis=-1).astype(
        jnp.bfloat16
    )
    query_slice = prepared[..., :head_dim]
    key_slice = prepared[..., head_dim : 2 * head_dim]
    value_slice = prepared[..., 2 * head_dim : 3 * head_dim]
    attention_logits = jnp.einsum(
        "ldg,bdg->dlb", query_slice, key_slice, preferred_element_type=jnp.float32
    ) * (1.0 / math.sqrt(head_dim))
    exponent_scores = jnp.exp(attention_logits)
    softmax_total = jnp.sum(exponent_scores, axis=-1)
    attention_output = jnp.einsum(
        "jdl,ljg->djg",
        exponent_scores.astype(jnp.bfloat16),
        value_slice,
        preferred_element_type=jnp.float32,
    )
    attention_output = attention_output / jnp.transpose(softmax_total)[:, :, None]
    blended_rows = jnp.concatenate(
        [attention_output.astype(jnp.bfloat16), prepared[..., 3 * head_dim :]], axis=-1
    )
    combined_output = lax.all_gather(out_local, "frames", axis=1, tiled=True)
    summed = lax.psum_scatter(
        jnp.einsum(
            "vto,ox->vtx", blended_rows, combined_output, preferred_element_type=jnp.float32
        ).astype(jnp.bfloat16),
        "tensor",
        scatter_dimension=0,
        tiled=True,
    ).astype(jnp.float32)
    return (patches.astype(jnp.float32) + summed).astype(jnp.bfloat16)


def solution(mesh):
    return jax.shard_map(
        local,
        mesh=mesh,
        in_specs=(
            P("tensor", ("groups", "frames"), None),
            P(),
            P("frames", "tensor", None),
            P("tensor", None),
            P("tensor", None),
            P("tensor", None, "frames"),
        ),
        out_specs=P("tensor", ("groups", "frames"), None),
        check_vma=False,
    )
```

profile of v0, /device:TPU:0, one launch (start us, length us, event | category | flops | bytes accessed | tf_op | source)
XLA Modules:
  0.0 220.3 jit_solution(9089769881547310153)
XLA Ops:
  6.5 0.0 copy-start
  6.5 0.0 copy-start.1
  6.5 0.0 all-gather.6.cloned.1.call-start
  6.5 1.4 convert_reduce_fusion
  7.9 1.5 fusion.5
  9.5 0.0 copy-done
  9.5 0.0 copy-done.1
  9.5 1.2 fusion.7
  10.7 0.0 all-gather.6.cloned.1.call-update
  10.7 0.0 all-gather.8.cloned.1.call-start
  10.8 0.7 all-gather.8.cloned.1.call-update
  11.5 0.0 all-gather.10.cloned.1.call-start
  11.5 0.7 all-gather.10.cloned.1.call-update
  12.2 0.0 copy-start.2
  12.2 0.0 copy-start.3
  12.2 0.0 reduce-scatter.2.cloned.1.call-start
  12.3 64.8 %all-gather.6.cloned.1.call-done = bf16[256,2,3072]{2,0,1:T(8,128)(2,1)} async-done(((bf16[64,2,3072]{2,0,1:T(8,128)(2,1)}), bf16[256,2,3072]{2,0,1:T(8,128)(2,1)}) %all-gather.6.cloned.1.call-update) | async-done | bytes 3145744 | tf_op jit(solution)/shard_map/all_gather | solution.py:20
  77.0 37.7 %all-gather.8.cloned.1.call-done = bf16[3072,1,768]{2,0,1:T(8,128)(2,1)} async-done(((bf16[768,1,768]{2,0,1:T(8,128)(2,1)}), bf16[3072,1,768]{2,0,1:T(8,128)(2,1)}) %all-gather.8.cloned.1.call-update) | async-done | bytes 4718608 | tf_op jit(solution)/shard_map/all_gather | solution.py:24
  114.7 5.9 %fusion = f32[256,2,768]{2,0,1:T(8,128)S(1)} fusion(bf16[256,2,3072]{2,0,1:T(8,128)(2,1)} %all-gather.6.cloned.1.call-done, bf16[3072,1,768]{2,0,1:T(8,128)(2,1)} %all-gather.8.cloned.1.call-done), kind=kOutput, calls=%fused_computation | convolution fusion | flops 2415919104 | bytes 9437184 | tf_op jit(solution)/shard_map/qye,ea->qya/dot_general | solution.py:21
  120.6 0.2 slice_reduce_fusion.1
  120.8 0.4 multiply_reduce_fusion.1
  121.2 0.0 copy-done.2
  121.3 0.0 copy-done.3
  121.3 0.5 fusion.33
  121.8 0.3 fusion.11
  122.0 1.7 fusion.14
  123.8 21.1 %all-gather.10.cloned.1.call-done = bf16[1,512,3072]{2,1,0:T(8,128)(2,1)} async-done(((bf16[1,512,768]{2,1,0:T(8,128)(2,1)}), bf16[1,512,3072]{2,1,0:T(8,128)(2,1)}) %all-gather.10.cloned.1.call-update) | async-done | bytes 3145744 | tf_op jit(solution)/shard_map/all_gather | solution.py:52
  144.8 5.4 %convolution_convert_fusion = bf16[256,2,3072]{2,0,1:T(8,128)(2,1)} fusion(bf16[1,512,3072]{2,1,0:T(8,128)(2,1)} %all-gather.10.cloned.1.call-done, bf16[256,2,384]{2,0,1:T(8,128)(2,1)S(1)} %fusion.14, bf16[256,2,128]{2,0,1:T(8,128)(2,1)S(1)} %fusion.11), kind=kOutput, calls=%fused_computation.2 | convolution fusion | flops 1613234176 | bytes 6815744 | tf_op jit(solution)/shard_map/vto,ox->vtx/dot_general | solution.py:54
  150.2 0.0 reduce-scatter.2.cloned.1.call-update
  150.2 60.6 %reduce-scatter.2.cloned.1.call-done = bf16[64,2,3072]{2,0,1:T(8,128)(2,1)} async-done(((bf16[256,2,3072]{2,0,1:T(8,128)(2,1)}), bf16[64,2,3072]{2,0,1:T(8,128)(2,1)}) %reduce-scatter.2.cloned.1.call-update) | async-done | bytes 786448 | tf_op jit(solution)/shard_map/reduce_scatter | solution.py:53
  210.8 1.3 fusion.8
  212.1 1.7 copy.8
  (5 shorter events, 0.0 us)
Async XLA Ops:
  6.5 2.9 %copy-start = (bf16[64,2,3072]{2,1,0:T(2,128)(2,1)S(1)}, bf16[64,2,3072]{2,1,0:T(2,128)(2,1)}, u32[]{:S(2)}) copy-start(bf16[64,2,3072]{2,1,0:T(2,128)(2,1)} %param.6) | copy-start | bytes 2359300
  6.5 2.9 %copy-start.1 = (f32[3072]{0:T(1024)S(1)}, f32[3072]{0:T(1024)}, u32[]{:S(2)}) copy-start(f32[3072]{0:T(1024)} %param.7) | copy-start | bytes 36868
  6.5 70.5 %all-gather.6.cloned.1.call-start = ((), (), s32[]{:S(2)}) async-start(), calls=%async_computation.1 | async-start | bytes 3932160 | tf_op jit(solution)/shard_map/all_gather | solution.py:20
  10.7 104.0 %all-gather.8.cloned.1.call-start = ((), (), s32[]{:S(2)}) async-start(), calls=%async_computation.3 | async-start | bytes 5898240 | tf_op jit(solution)/shard_map/all_gather | solution.py:24
  11.5 133.3 %all-gather.10.cloned.1.call-start = ((), (), s32[]{:S(2)}) async-start(), calls=%async_computation.4 | async-start | bytes 3932160 | tf_op jit(solution)/shard_map/all_gather | solution.py:52
  12.2 109.0 %copy-start.2 = (f32[1,128]{1,0:T(1,128)S(1)}, f32[1,128]{1,0:T(1,128)}, u32[]{:S(2)}) copy-start(f32[1,128]{1,0:T(1,128)} %param.10) | copy-start | bytes 1540
  12.2 109.0 %copy-start.3 = (f32[1,128]{1,0:T(1,128)S(1)}, f32[1,128]{1,0:T(1,128)}, u32[]{:S(2)}) copy-start(f32[1,128]{1,0:T(1,128)} %param.9) | copy-start | bytes 1540
  12.2 198.5 %reduce-scatter.2.cloned.1.call-start = ((), (), s32[]{:S(2)}) async-start(), calls=%async_computation.2 | async-start | bytes 3932160 | tf_op jit(solution)/shard_map/reduce_scatter | solution.py:53
Sparse Core Ops, SparseCore 0:
  10.8 66.1 all-gather.5
  78.6 36.0 all-gather.7
  116.3 28.5 all-gather.9
  150.3 60.3 reduce-scatter.1
where the time goes:
time: 221 us; the launch traced here: 220 us
  waiting for transfers between devices  185 us (84%)
  between operations  13.2 us (6%)
  matrix products  12 us (5%)
  other arithmetic  7.81 us (4%)
    all_gather x1, waiting for transfers between devices, local(): every_patch = lax.all_gather(normed, 'tensor', axis=0, tiled=True)  64.8 us
    reduce_scatter x1, waiting for transfers between devices, local(): lax.psum_scatter(jnp.einsum('vto,ox->vtx', blended_rows, combined_output,...  60.6 us
    all_gather x1, waiting for transfers between devices, local(): lax.all_gather(in_local, 'frames', axis=0, tiled=True)  37.7 us
    all_gather x1, waiting for transfers between devices, local(): combined_output = lax.all_gather(out_local, 'frames', axis=1, tiled=True)  21.1 us
    dot_general x1, matrix products, local(): jnp.einsum('qye,ea->qya', every_patch, lax.all_gather(in_local, 'frames',...  5.89 us
    dot_general x1, matrix products, local(): jnp.einsum('vto,ox->vtx', blended_rows, combined_output, preferred_elemen...  5.36 us
  transfers between devices with their start and end apart: 4, of which 4 were waited for; matrix products, arithmetic and copies ran while one was open for 4% of the time, Pallas kernels for 0%

commit v1 on v0

--- a/solution.py
+++ b/solution.py
@@ -18,12 +18,22 @@
     in_local = in_weight[:, 0, :]
     out_local = out_weight[0]
     every_patch = lax.all_gather(normed, "tensor", axis=0, tiled=True)
-    joined_cols = jnp.einsum(
-        "qye,ea->qya",
-        every_patch,
-        lax.all_gather(in_local, "frames", axis=0, tiled=True),
-        preferred_element_type=jnp.float32,
-    )
+    size, here, span = (lax.axis_size("frames"), lax.axis_index("frames"), in_local.shape[0])
+    ahead = [(i, (i + 1) % size) for i in range(size)]
+    held, total = (in_local, None)
+    for turn in range(size):
+        coming = lax.ppermute(held, "frames", ahead) if turn < size - 1 else None
+        update = jnp.einsum(
+            "qye,ea->qya",
+            lax.dynamic_slice_in_dim(
+                every_patch, (here - turn) % size * span, held.shape[0], axis=2
+            ),
+            held,
+            preferred_element_type=jnp.float32,
+        )
+        total = update if total is None else total + update
+        held = coming
+    joined_cols = total
     query_slice = layer_norm(joined_cols[..., :head_dim], q_gain[0])
     key_slice = layer_norm(joined_cols[..., head_dim : 2 * head_dim], k_gain[0])
     value_slice = joined_cols[..., 2 * head_dim : 3 * head_dim]

time: 221 us -> 182 us (0.82)
  waiting for transfers between devices: 185 us -> 145 us
    all_gather x1 -> x0, waiting for transfers between devices: 37.7 us -> none  [local(): lax.all_gather(in_local, 'frames', axis=0, tiled=True)]
    all_gather x1, waiting for transfers between devices: 64.8 us -> 34.2 us  [local(): every_patch = lax.all_gather(normed, 'tensor', axis=0, tiled=True)]
    ppermute x0 -> x3, waiting for transfers between devices: none -> 30.5 us  [local(): coming = lax.ppermute(held, 'frames', ahead) if turn < size - 1 else None]
    dot_general x1 -> x4, matrix products: 5.89 us -> 6.11 us  [local(): jnp.einsum('qye,ea->qya', lax.dynamic_slice_in_dim(every_patch, (here - t...]
  transfers between devices with their start and end apart: 4 -> 6, of which waited for: 4 -> 5; matrix products, arithmetic and copies ran while one was open for 4% -> 5% of each run, Pallas kernels for 0% -> 0%
where the time goes in v1:
time: 182 us; the launch traced here: 181 us
  waiting for transfers between devices  145 us (80%)
  between operations  13.2 us (7%)
  matrix products  12.3 us (7%)
  other arithmetic  7.9 us (4%)
  local copies, waits for them, and re-layouts  2.73 us (2%)
    reduce_scatter x1, waiting for transfers between devices, local(): lax.psum_scatter(jnp.einsum('vto,ox->vtx', blended_rows, combined_output,...  60.6 us
    all_gather x1, waiting for transfers between devices, local(): every_patch = lax.all_gather(normed, 'tensor', axis=0, tiled=True)  34.2 us
    ppermute x3, waiting for transfers between devices, local(): coming = lax.ppermute(held, 'frames', ahead) if turn < size - 1 else None  30.5 us
    all_gather x1, waiting for transfers between devices, local(): combined_output = lax.all_gather(out_local, 'frames', axis=1, tiled=True)  19.4 us
    dot_general x4, matrix products, local(): jnp.einsum('qye,ea->qya', lax.dynamic_slice_in_dim(every_patch, (here - t...  6.11 us
    dot_general x1, matrix products, local(): jnp.einsum('vto,ox->vtx', blended_rows, combined_output, preferred_elemen...  5.39 us
  transfers between devices with their start and end apart: 6, of which 5 were waited for; matrix products, arithmetic and copies ran while one was open for 5% of the time, Pallas kernels for 0%

profile of v1, /device:TPU:0, one launch (start us, length us, event | category | flops | bytes accessed | tf_op | source)
XLA Modules:
  0.0 181.4 jit_solution(5927086848049520350)
XLA Ops:
  6.5 0.0 copy-start
  6.5 0.0 copy-start.2
  6.5 0.0 all-gather.4.cloned.1.call-start
  6.5 1.4 convert_reduce_fusion
  7.9 0.0 copy-start.3
  8.0 1.6 fusion.3
  9.6 0.0 copy-done
  9.6 0.0 copy-done.2
  9.6 1.2 fusion.5
  10.8 0.0 all-gather.4.cloned.1.call-update
  10.8 0.0 all-gather.6.cloned.1.call-start
  10.9 0.0 copy-done.3
  10.9 0.5 collective-permute-start
  11.4 15.8 %collective-permute-done = bf16[768,768]{1,0:T(8,128)(2,1)S(1)} collective-permute-done((bf16[768,768]{1,0:T(8,128)(2,1)S(1)}, bf16[768,768]{1,0:T(8,128)(2,1)S(1)}, u32[]{:S(2)}, u32[]{:S(2)}) %collective-permute-start) | collective-permute-done | bytes 1179680 | tf_op jit(solution)/shard_map/ppermute | solution.py:25
  27.2 0.0 copy-start.4
  27.2 0.0 collective-permute-start.1
  27.2 0.0 all-gather.6.cloned.1.call-update
  27.3 0.0 reduce-scatter.2.cloned.1.call-start
  27.3 1.0 copy-done.4
  28.3 14.7 %collective-permute-done.1 = bf16[768,768]{1,0:T(8,128)(2,1)} collective-permute-done((bf16[768,768]{1,0:T(8,128)(2,1)S(1)}, bf16[768,768]{1,0:T(8,128)(2,1)}, u32[]{:S(2)}, u32[]{:S(2)}) %collective-permute-start.1) | collective-permute-done | bytes 1179680 | tf_op jit(solution)/shard_map/ppermute | solution.py:25
  43.0 0.0 collective-permute-start.2
  43.0 34.2 %all-gather.4.cloned.1.call-done = bf16[256,2,3072]{2,0,1:T(8,128)(2,1)} async-done(((bf16[64,2,3072]{2,0,1:T(8,128)(2,1)}), bf16[256,2,3072]{2,0,1:T(8,128)(2,1)}) %all-gather.4.cloned.1.call-update) | async-done | bytes 3145744 | tf_op jit(solution)/shard_map/all_gather | solution.py:20
  77.1 0.0 copy-start.1
  77.1 2.4 %fusion.9 = f32[256,2,768]{2,0,1:T(8,128)S(1)} fusion(bf16[768,768]{1,0:T(8,128)(2,1)} %collective-permute-done.1, bf16[256,2,3072]{2,0,1:T(8,128)(2,1)} %all-gather.4.cloned.1.call-done, s32[]{:T(128)S(6)} %select_n.36), kind=kOutput, calls=%fused_computation.16 | convolution fusion | flops 603979776 | bytes 3538948 | tf_op jit(solution)/shard_map/qye,ea->qya/dot_general | solution.py:26
  79.6 0.0 copy-done.1
  79.6 2.1 %fusion.11 = f32[256,2,768]{2,0,1:T(8,128)S(1)} fusion(bf16[768,768]{1,0:T(8,128)(2,1)} %copy-done.4, bf16[256,2,3072]{2,0,1:T(8,128)(2,1)S(1)} %copy-done.1, s32[]{:T(128)S(6)} %select_n.34), kind=kOutput, calls=%fused_computation.18 | convolution fusion | flops 603979776 | bytes 3538948 | tf_op jit(solution)/shard_map/qye,ea->qya/dot_general | solution.py:26
  81.7 0.8 fusion.13
  82.5 0.0 copy-start.5
  82.5 0.0 copy-start.6
  82.5 0.0 collective-permute-done.2
  82.5 0.8 add_add_fusion
  83.3 0.2 slice_reduce_fusion.1
  83.6 0.4 multiply_reduce_fusion.1
  84.0 0.0 copy-done.5
  84.0 0.0 copy-done.6
  84.0 0.5 fusion.46
  84.5 0.3 fusion.16
  84.8 1.7 fusion.19
  86.5 19.4 %all-gather.6.cloned.1.call-done = bf16[1,512,3072]{2,1,0:T(8,128)(2,1)} async-done(((bf16[1,512,768]{2,1,0:T(8,128)(2,1)}), bf16[1,512,3072]{2,1,0:T(8,128)(2,1)}) %all-gather.6.cloned.1.call-update) | async-done | bytes 3145744 | tf_op jit(solution)/shard_map/all_gather | solution.py:62
  105.9 5.4 %convolution_convert_fusion = bf16[256,2,3072]{2,0,1:T(8,128)(2,1)} fusion(bf16[1,512,3072]{2,1,0:T(8,128)(2,1)} %all-gather.6.cloned.1.call-done, bf16[256,2,384]{2,0,1:T(8,128)(2,1)S(1)} %fusion.19, bf16[256,2,128]{2,0,1:T(8,128)(2,1)S(1)} %fusion.16), kind=kOutput, calls=%fused_computation | convolution fusion | flops 1613234176 | bytes 6815744 | tf_op jit(solution)/shard_map/vto,ox->vtx/dot_general | solution.py:64
  111.3 0.0 reduce-scatter.2.cloned.1.call-update
  111.3 60.6 %reduce-scatter.2.cloned.1.call-done = bf16[64,2,3072]{2,0,1:T(8,128)(2,1)} async-done(((bf16[256,2,3072]{2,0,1:T(8,128)(2,1)}), bf16[64,2,3072]{2,0,1:T(8,128)(2,1)}) %reduce-scatter.2.cloned.1.call-update) | async-done | bytes 786448 | tf_op jit(solution)/shard_map/reduce_scatter | solution.py:63
  171.9 1.3 fusion.6
  173.2 1.7 copy.8
  (5 shorter events, 0.0 us)
Async XLA Ops:
  6.5 3.0 %copy-start = (bf16[64,2,3072]{2,1,0:T(2,128)(2,1)S(1)}, bf16[64,2,3072]{2,1,0:T(2,128)(2,1)}, u32[]{:S(2)}) copy-start(bf16[64,2,3072]{2,1,0:T(2,128)(2,1)} %param.6) | copy-start | bytes 2359300
  6.5 3.0 %copy-start.2 = (f32[3072]{0:T(1024)S(1)}, f32[3072]{0:T(1024)}, u32[]{:S(2)}) copy-start(f32[3072]{0:T(1024)} %param.7) | copy-start | bytes 36868
  6.5 70.6 %all-gather.4.cloned.1.call-start = ((), (), s32[]{:S(2)}) async-start(), calls=%async_computation.1 | async-start | bytes 3932160 | tf_op jit(solution)/shard_map/all_gather | solution.py:20
  7.9 2.9 %copy-start.3 = (bf16[768,1,768]{2,0,1:T(8,128)(2,1)S(1)}, bf16[768,1,768]{2,0,1:T(8,128)(2,1)}, u32[]{:S(2)}) copy-start(bf16[768,1,768]{2,0,1:T(8,128)(2,1)} %param.8) | copy-start | bytes 3538948
  10.8 95.1 %all-gather.6.cloned.1.call-start = ((), (), s32[]{:S(2)}) async-start(), calls=%async_computation.3 | async-start | bytes 3932160 | tf_op jit(solution)/shard_map/all_gather | solution.py:62
  10.9 16.3 %collective-permute-start = (bf16[768,768]{1,0:T(8,128)(2,1)S(1)}, bf16[768,768]{1,0:T(8,128)(2,1)S(1)}, u32[]{:S(2)}, u32[]{:S(2)}) collective-permute-start(bf16[768,768]{1,0:T(8,128)(2,1)S(1)} %bitcast.27), channel_id=1, source_target_pairs={{0,1},{1,2},{2,3},{3,0},{4,5},{5,6},{6,7},{7,4},{8,9},{9,10},{10,1... | collective-permute-start | bytes 3538952 | tf_op jit(solution)/shard_map/ppermute | solution.py:25
  27.2 1.1 copy-start.4
  27.2 15.7 %collective-permute-start.1 = (bf16[768,768]{1,0:T(8,128)(2,1)S(1)}, bf16[768,768]{1,0:T(8,128)(2,1)}, u32[]{:S(2)}, u32[]{:S(2)}) collective-permute-start(bf16[768,768]{1,0:T(8,128)(2,1)S(1)} %collective-permute-done), channel_id=1, source_target_pairs={{0,1},{1,2},{2,3},{3,0},{4,5},{5,6},{6,7},{7,4},{8,9},{9,10},{10,1... | collective-permute-start | bytes 3538952 | tf_op jit(solution)/shard_map/ppermute | solution.py:25
  27.3 144.6 %reduce-scatter.2.cloned.1.call-start = ((), (), s32[]{:S(2)}) async-start(), calls=%async_computation.2 | async-start | bytes 3932160 | tf_op jit(solution)/shard_map/reduce_scatter | solution.py:63
  43.0 39.5 %collective-permute-start.2 = (bf16[768,768]{1,0:T(8,128)(2,1)}, bf16[768,768]{1,0:T(8,128)(2,1)S(1)}, u32[]{:S(2)}, u32[]{:S(2)}) collective-permute-start(bf16[768,768]{1,0:T(8,128)(2,1)} %collective-permute-done.1), channel_id=1, source_target_pairs={{0,1},{1,2},{2,3},{3,0},{4,5},{5,6},{6,7},{7,4},{8,9},{9,10},{10,1... | collective-permute-start | bytes 3538952 | tf_op jit(solution)/shard_map/ppermute | solution.py:25
  77.1 2.5 %copy-start.1 = (bf16[256,2,3072]{2,0,1:T(8,128)(2,1)S(1)}, bf16[256,2,3072]{2,0,1:T(8,128)(2,1)}, u32[]{:S(2)}) copy-start(bf16[256,2,3072]{2,0,1:T(8,128)(2,1)} %all-gather.4.cloned.1.call-done) | copy-start | bytes 9437188
  82.5 1.5 copy-start.5
  82.5 1.5 copy-start.6
Sparse Core Ops, SparseCore 0:
  10.9 66.1 all-gather.3
  78.7 27.1 all-gather.5
  111.4 60.3 reduce-scatter.1
